TPU v7x, 8 devices: a whole 2x2x1 slice. The times are simulated.
8 devices in a mesh: col: 2 (over z, y), row: 4 (over x, core).
Axes of the slice: x: 2, y: 2, z: 1, core: 2. Of those that a mesh axis runs over, the one named last changes fastest.
Arguments:
- img_emb: bfloat16 [8192, 512], P(('row', 'col'))
- txt_emb: bfloat16 [8192, 512], P(('row', 'col'))
- log_scale: float32 [], replicated
Outputs:
- output 1: float32 [], replicated
- output 2: bfloat16 [8192, 512], P(('row', 'col'))
- output 3: bfloat16 [8192, 512], P(('row', 'col'))
- output 4: float32 [], replicated
All inputs are finite; a program needn't handle non-finite values.
Results may differ from a plain program's by a relative error of at most 0.001.
Values are sent between devices in bfloat16 or wider.
A program may use at most 1 GiB of HBM per device.

v0:
```python
import jax
import jax.numpy as jnp
from jax import lax
from jax.sharding import PartitionSpec as P, NamedSharding


def solution(mesh):
    n_row = mesh.shape["row"]
    n_col = mesh.shape["col"]
    batch_spec = P(("row", "col"), None)
    both_axes = ("row", "col")

    def local_tile(img_loc, txt_loc, log_scale):
        rows_dev = img_loc.shape[0]
        batch_size = rows_dev * n_row * n_col
        inv_count = 1.0 / (2 * batch_size)
        row_id = lax.axis_index("row")
        col_id = lax.axis_index("col")
        logit_scale = jnp.exp(log_scale)
        img_block = lax.all_gather(img_loc, "col", tiled=True)
        txt_block = lax.all_gather(txt_loc, "row", tiled=True)
        logits = logit_scale * jnp.einsum("id,jd->ij", img_block, txt_block, preferred_element_type=jnp.float32)
        row_glob = row_id * (rows_dev * n_col) + jnp.arange(rows_dev * n_col)
        col_pos = jnp.arange(rows_dev * n_row)
        col_glob = ((col_pos // rows_dev) * n_col + col_id) * rows_dev + col_pos % rows_dev
        diag_mask = row_glob[:, None] == col_glob[None, :]
        row_max = jnp.max(logits, axis=1)
        row_exp = jnp.exp(logits - row_max[:, None])
        row_part = jnp.sum(row_exp, axis=1)
        col_max = jnp.max(logits, axis=0)
        col_exp = jnp.exp(logits - col_max[None, :])
        col_part = jnp.sum(col_exp, axis=0)
        row_top = lax.pmax(row_max, "col")
        row_tot = lax.psum(row_part * jnp.exp(row_max - row_top), "col")
        row_lse = row_top + jnp.log(row_tot)
        col_top = lax.pmax(col_max, "row")
        col_tot = lax.psum(col_part * jnp.exp(col_max - col_top), "row")
        col_lse = col_top + jnp.log(col_tot)
        own_block = lax.dynamic_slice(logits, (col_id * rows_dev, row_id * rows_dev), (rows_dev, rows_dev))
        own_diag = jnp.diagonal(own_block)
        own_row_lse = lax.dynamic_slice(row_lse, (col_id * rows_dev,), (rows_dev,))
        own_col_lse = lax.dynamic_slice(col_lse, (row_id * rows_dev,), (rows_dev,))
        loss_part = jnp.sum(own_row_lse + own_col_lse - 2.0 * own_diag)
        total_loss = lax.psum(loss_part, both_axes) * inv_count
        row_factor = jnp.exp(row_max - row_lse) * inv_count
        col_factor = jnp.exp(col_max - col_lse) * inv_count
        grad_tile = row_exp * row_factor[:, None] + col_exp * col_factor[None, :] - jnp.where(diag_mask, 2.0 * inv_count, 0.0)
        d_log_scale = lax.psum(jnp.sum(grad_tile * logits), both_axes)
        grad_bf = grad_tile.astype(jnp.bfloat16)
        img_part = jnp.einsum("ij,jd->id", grad_bf, txt_block, preferred_element_type=jnp.float32)
        img_sum = lax.psum_scatter(img_part, "col", scatter_dimension=0, tiled=True)
        d_img = (logit_scale * img_sum).astype(jnp.bfloat16)
        txt_part = jnp.einsum("ij,id->jd", grad_bf, img_block, preferred_element_type=jnp.float32)
        txt_sum = lax.psum_scatter(txt_part, "row", scatter_dimension=0, tiled=True)
        d_txt = (logit_scale * txt_sum).astype(jnp.bfloat16)
        return total_loss, d_img, d_txt, d_log_scale

    return jax.shard_map(local_tile, mesh=mesh, in_specs=(batch_spec, batch_spec, P()), out_specs=(P(), batch_spec, batch_spec, P()), check_vma=False)
```

profile of v0, /device:TPU:0, one launch (start us, length us, event | category | flops | bytes accessed | tf_op | source)
XLA Modules:
  0.0 308.2 jit_solution(16010651862951946728)
XLA Ops:
  7.2 0.0 all-gather.3.cloned.1.call-start
  7.2 0.7 all-gather.3.cloned.1.call-update
  7.9 0.0 all-gather.5.cloned.1.call-start
  7.9 0.7 all-gather.5.cloned.1.call-update
  8.6 0.0 reduce-scatter.3.cloned.1.call-start
  9.4 33.1 %all-gather.3.cloned.1.call-done = bf16[2048,512]{1,0:T(8,128)(2,1)} async-done(((bf16[1024,512]{1,0:T(8,128)(2,1)}), bf16[2048,512]{1,0:T(8,128)(2,1)}) %all-gather.3.cloned.1.call-update) | async-done | bytes 2097168 | tf_op jit(solution)/shard_map/all_gather | solution.py:20
  42.5 33.1 %all-gather.5.cloned.1.call-done = bf16[4096,512]{1,0:T(8,128)(2,1)} async-done(((bf16[1024,512]{1,0:T(8,128)(2,1)}), bf16[4096,512]{1,0:T(8,128)(2,1)}) %all-gather.5.cloned.1.call-update) | async-done | bytes 4194320 | tf_op jit(solution)/shard_map/all_gather | solution.py:21
  75.5 17.8 %fusion.14 = (f32[2048]{0:T(1024)S(1)}, f32[4096]{0:T(1024)S(1)}, f32[2048,4096]{1,0:T(8,128)}) fusion(bf16[2048,512]{1,0:T(8,128)(2,1)} %all-gather.3.cloned.1.call-done, bf16[4096,512]{1,0:T(8,128)(2,1)} %all-gather.5.cloned.1.call-done, f32[]{:T(128)S(6)} %exp.21), kind=kOutput, calls=%fused_computation.35 | convolution fusion | flops 8615094272 | bytes 39870468 | tf_op jit(solution)/shard_map/id,jd->ij/dot_general | solution.py:22
  93.3 10.2 %pmax.15 = f32[4096]{0:T(1024)S(1)} all-reduce(f32[4096]{0:T(1024)S(1)} %get-tuple-element.7), channel_id=1, replica_groups=mesh['col'=2,'row'=4] {'row'}, use_global_device_ids=true, to_apply=%region_5.6 | all-reduce | flops 4096 | bytes 32768 | tf_op jit(solution)/shard_map/pmax | solution.py:36
  103.6 5.0 %pmax.14 = f32[2048]{0:T(1024)S(1)} all-reduce(f32[2048]{0:T(1024)S(1)} %get-tuple-element.6), channel_id=1, replica_groups=mesh['col'=2,'row'=4] {'col'}, use_global_device_ids=true, to_apply=%region_1.2 | all-reduce | flops 2048 | bytes 16384 | tf_op jit(solution)/shard_map/pmax | solution.py:33
  108.5 15.5 %fusion = (f32[2048]{0:T(1024)S(1)}, f32[4096]{0:T(1024)S(1)}) fusion(f32[2048,4096]{1,0:T(8,128)} %get-tuple-element.16, f32[2048]{0:T(1024)S(1)} %get-tuple-element.6, f32[4096]{0:T(1024)S(1)} %get-tuple-element.7), kind=kLoop, calls=%fused_computation.5 | loop fusion | flops 33548288 | bytes 33603584 | tf_op jit(solution)/shard_map/reduce_sum | solution.py:29
  124.1 10.1 %psum.29 = f32[4096]{0:T(1024)S(1)} all-reduce(f32[4096]{0:T(1024)S(1)} %exponential_multiply_fusion.1), channel_id=1, replica_groups=mesh['col'=2,'row'=4] {'row'}, use_global_device_ids=true, to_apply=%region_7.8 | all-reduce | flops 4096 | bytes 32768 | tf_op jit(solution)/shard_map/psum | solution.py:37
  134.2 5.0 %psum.28 = f32[2048]{0:T(1024)S(1)} all-reduce(f32[2048]{0:T(1024)S(1)} %exponential_multiply_fusion.3), channel_id=1, replica_groups=mesh['col'=2,'row'=4] {'col'}, use_global_device_ids=true, to_apply=%region_3.4 | all-reduce | flops 2048 | bytes 16384 | tf_op jit(solution)/shard_map/psum | solution.py:34
  139.2 0.0 copy-start.1
  139.2 21.2 %fusion.2 = (bf16[2048,4096]{1,0:T(8,128)(2,1)S(1)}, f32[]{:T(128)}) fusion(f32[2048,4096]{1,0:T(8,128)} %get-tuple-element.16, s32[4096]{0:T(1024)S(1)} %fusion.12, f32[4096]{0:T(1024)S(1)} %get-tuple-element.12, f32[2048]{0:T(1024)S(1)} %get-tuple-element.10, f32[4096]{0:T(1024)S(1)} %get-tuple-element.7, f32[2048]{0:T(1024)S(1)} %get-tuple-element.6, ...), kind=kLoop, calls=%fused_computation.7 | loop fusion | flops 92274688 | bytes 50405380 | tf_op jit(solution)/shard_map/convert_element_type | solution.py:49
  160.5 0.0 copy-start
  160.5 5.7 %copy-done = bf16[2048,4096]{1,0:T(8,128)(2,1)} copy-done((bf16[2048,4096]{1,0:T(8,128)(2,1)}, bf16[2048,4096]{1,0:T(8,128)(2,1)S(1)}, u32[]{:S(2)}) %copy-start) | copy-done | bytes 16777240
  166.2 0.0 copy-done.1
  166.2 0.0 copy-start.2
  166.2 10.3 %fusion.15 = f32[2048,512]{1,0:T(8,128)} fusion(bf16[2048,4096]{1,0:T(8,128)(2,1)S(1)} %get-tuple-element.14, bf16[4096,512]{1,0:T(8,128)(2,1)S(1)} %copy-done.1), kind=kOutput, calls=%fused_computation.36 | convolution fusion | flops 8589934592 | bytes 25165824 | tf_op jit(solution)/shard_map/ij,jd->id/dot_general | solution.py:50
  176.4 0.0 reduce-scatter.3.cloned.1.call-update
  176.5 0.2 reduce-scatter.5.cloned.1.call-start
  176.7 0.0 copy-done.2
  176.7 14.5 %fusion.16 = f32[4096,512]{1,0:T(8,128)} fusion(bf16[2048,4096]{1,0:T(8,128)(2,1)} %copy-done, bf16[2048,512]{1,0:T(8,128)(2,1)S(1)} %copy-done.2), kind=kOutput, calls=%fused_computation.37 | convolution fusion | flops 8589934592 | bytes 27262976 | tf_op jit(solution)/shard_map/ij,id->jd/dot_general | solution.py:53
  191.2 0.0 reduce-scatter.5.cloned.1.call-update
  191.2 4.8 %dynamic_slice.11 = f32[1024,1024]{1,0:T(8,128)} dynamic-slice(f32[2048,4096]{1,0:T(8,128)} %get-tuple-element.16, s32[]{:T(128)S(6)} %select_n.36, s32[]{:T(128)S(6)} %select_n.37), dynamic_slice_sizes={1024,1024} | dynamic-slice | bytes 8388612 | tf_op jit(solution)/shard_map/dynamic_slice | solution.py:39
  196.0 16.6 %gather_fusion = f32[1024]{0:T(1024)S(1)} fusion(f32[1024,1024]{1,0:T(8,128)} %dynamic_slice.11, s32[1024]{0:T(1024)S(1)} %bitcast.7), kind=kCustom, calls=%fused_computation | custom fusion | bytes 16384 | tf_op jit(solution)/shard_map/jit(diagonal)/cond/branch_0_fun/gather | solution.py:40
  212.7 0.6 subtract_reduce_fusion
  213.3 24.0 %all-reduce = (f32[]{:T(128)}, f32[]{:T(128)}) all-reduce(f32[]{:T(128)} %subtract_reduce_fusion, f32[]{:T(128)} %get-tuple-element.15), channel_id=1, replica_groups=mesh['col'=2,'row'=4] {'row','col'}, use_global_device_ids=true, to_apply=%region_9.10 | all-reduce | flops 2 | bytes 16 | tf_op jit(solution)/shard_map/psum | solution.py:44
  238.0 0.0 reduce-scatter.3.cloned.1.call-done
  238.0 2.8 multiply_convert_fusion.1
  240.8 56.9 %reduce-scatter.5.cloned.1.call-done = f32[1024,512]{1,0:T(8,128)} async-done(((f32[4096,512]{1,0:T(8,128)}), f32[1024,512]{1,0:T(8,128)}) %reduce-scatter.5.cloned.1.call-update) | async-done | bytes 2097168 | tf_op jit(solution)/shard_map/reduce_scatter | solution.py:54
  297.7 2.8 multiply_convert_fusion
  (7 shorter events, 0.1 us)
Async XLA Ops:
  7.2 35.3 %all-gather.3.cloned.1.call-start = ((), (), s32[]{:S(2)}) async-start(), calls=%async_computation.2 | async-start | bytes 3145728 | tf_op jit(solution)/shard_map/all_gather | solution.py:20
  7.9 67.6 %all-gather.5.cloned.1.call-start = ((), (), s32[]{:S(2)}) async-start(), calls=%async_computation.3 | async-start | bytes 5242880 | tf_op jit(solution)/shard_map/all_gather | solution.py:21
  8.6 229.3 %reduce-scatter.3.cloned.1.call-start = ((), (), s32[]{:S(2)}) async-start(), calls=%async_computation.4 | async-start | bytes 6291456 | tf_op jit(solution)/shard_map/reduce_scatter | solution.py:51
  139.2 26.9 %copy-start.1 = (bf16[4096,512]{1,0:T(8,128)(2,1)S(1)}, bf16[4096,512]{1,0:T(8,128)(2,1)}, u32[]{:S(2)}) copy-start(bf16[4096,512]{1,0:T(8,128)(2,1)} %all-gather.5.cloned.1.call-done) | copy-start | bytes 12582916
  160.5 5.7 %copy-start = (bf16[2048,4096]{1,0:T(8,128)(2,1)}, bf16[2048,4096]{1,0:T(8,128)(2,1)S(1)}, u32[]{:S(2)}) copy-start(bf16[2048,4096]{1,0:T(8,128)(2,1)S(1)} %get-tuple-element.14) | copy-start | bytes 50331652
  166.2 10.5 %copy-start.2 = (bf16[2048,512]{1,0:T(8,128)(2,1)S(1)}, bf16[2048,512]{1,0:T(8,128)(2,1)}, u32[]{:S(2)}) copy-start(bf16[2048,512]{1,0:T(8,128)(2,1)} %all-gather.3.cloned.1.call-done) | copy-start | bytes 6291460
  176.5 121.2 %reduce-scatter.5.cloned.1.call-start = ((), (), s32[]{:S(2)}) async-start(), calls=%async_computation.5 | async-start | bytes 10485760 | tf_op jit(solution)/shard_map/reduce_scatter | solution.py:54
Sparse Core Ops, SparseCore 0:
  9.5 32.9 all-gather.2
  44.0 31.4 all-gather.4
  176.6 53.4 reduce-scatter.2
  232.5 65.1 reduce-scatter.4
where the time goes:
time: 309 us; the launch traced here: 308 us
  waiting for transfers between devices  124 us (40%)
  blocking collectives  54.3 us (18%)
  other arithmetic  43.1 us (14%)
  matrix products  42.5 us (14%)
  local copies, waits for them, and re-layouts  27.2 us (9%)
  between operations  16.3 us (5%)
    reduce_scatter x1, waiting for transfers between devices, local_tile(): txt_sum = lax.psum_scatter(txt_part, 'row', scatter_dimension=0, tiled=True)  56.9 us
    all_gather x1, waiting for transfers between devices, local_tile(): img_block = lax.all_gather(img_loc, 'col', tiled=True)  33.1 us
    all_gather x1, waiting for transfers between devices, local_tile(): txt_block = lax.all_gather(txt_loc, 'row', tiled=True)  33.1 us
    psum x1, blocking collectives, local_tile(): total_loss = lax.psum(loss_part, both_axes) * inv_count  24 us
    convert_element_type x1, other arithmetic, local_tile(): grad_bf = grad_tile.astype(jnp.bfloat16)  21.2 us
    dot_general x1, matrix products, local_tile(): jnp.einsum('id,jd->ij', img_block, txt_block, preferred_element_type=jnp....  17.8 us
    gather x1, local copies, waits for them, and re-layouts, local_tile(): own_diag = jnp.diagonal(own_block)  16.6 us
    reduce_sum x1, other arithmetic, local_tile(): row_part = jnp.sum(row_exp, axis=1)  15.5 us
  transfers between devices with their start and end apart: 4, of which 3 were waited for; matrix products, arithmetic and copies ran while one was open for 13% of the time, Pallas kernels for 0%

commit v1 on v0

v1 whole, which is shorter than its diff:
```python
import functools
import math

import jax
import jax.numpy as jnp
from jax import lax
from jax.experimental import pallas as pl
from jax.experimental.pallas import tpu as pltpu
from jax.sharding import PartitionSpec as P

MESH = pl.DeviceIdType.MESH
F32 = jnp.float32
BF16 = jnp.bfloat16
ROWS = 1024
DIM = 512
CHUNK = 256
STEPS = ROWS // CHUNK
IMGS = 2 * ROWS
TXTS = 4 * ROWS
LOG2E = math.log2(math.e)


def kernel(inv_count, scale_ref, img_hbm, txt_hbm, loss_ref, dimg_hbm, dtxt_hbm, dscale_ref,
           img, txt, exps, row_e, row_m, col_e, col_m, row_send, row_recv, col_send, col_recv, col_b,
           g_row, g_col, d_img_send, d_img_recv, d_img_own, ring, d_txt_x, d_txt_p, d_txt_recv, d_txt_own, out_stage,
           scal, scal_y, load_sem, gy_send, gy_recv, gx_send, gx_recv, gp_sem, gf_send, gf_recv, row_sem, col_ssem, col_rsem,
           ry_send, ry_recv, rp_send, rp_recv, rx_send, rx_recv, sc_ssem, sc_rsem, out_sem):
    row = lax.axis_index("row")
    col = lax.axis_index("col")
    core = lax.rem(row, 2)
    partner = row + 1 - 2 * core
    across = lax.rem(row + 2, 4)
    diagonal = across + 1 - 2 * core
    peers = (partner, across, diagonal)
    other_col = 1 - col

    def to_y(src, dst, ssem, rsem):
        return pltpu.make_async_remote_copy(src, dst, ssem, rsem, device_id={"row": row, "col": other_col}, device_id_type=MESH)

    def to_row(src, dst, ssem, rsem, peer):
        return pltpu.make_async_remote_copy(src, dst, ssem, rsem, device_id={"row": peer, "col": col}, device_id_type=MESH)

    load_img = pltpu.make_async_copy(img_hbm, img.at[pl.ds(0, ROWS)], load_sem.at[0])
    load_txt = pltpu.make_async_copy(txt_hbm, txt.at[pl.ds(0, ROWS)], load_sem.at[1])
    load_img.start()
    load_txt.start()

    barrier = pltpu.get_barrier_semaphore()
    for peer in peers:
        pl.semaphore_signal(barrier, inc=1, device_id={"row": peer, "col": col}, device_id_type=MESH)
    pl.semaphore_signal(barrier, inc=1, device_id={"row": row, "col": other_col}, device_id_type=MESH)

    scale = jnp.max(jnp.exp(jnp.full((8, 128), scale_ref[0, 0], F32)))
    scale2 = scale * LOG2E
    row_e[...] = jnp.zeros_like(row_e)
    row_m[...] = jnp.zeros_like(row_m)
    col_e[...] = jnp.zeros_like(col_e)
    col_m[...] = jnp.zeros_like(col_m)

    load_img.wait()
    load_txt.wait()
    pl.semaphore_wait(barrier, 4)

    gather_y, gather_x = [], []
    for k in range(STEPS):
        part = pl.ds(k * CHUNK, CHUNK)
        gather_x.append(to_row(txt.at[part], txt.at[pl.ds(2 * ROWS + k * CHUNK, CHUNK)], gx_send.at[k], gx_recv.at[k], across))
        gather_y.append(to_y(img.at[part], img.at[pl.ds(ROWS + k * CHUNK, CHUNK)], gy_send.at[k], gy_recv.at[k]))
        gather_x[k].start()
        gather_y[k].start()
    gather_p = to_row(txt.at[pl.ds(0, ROWS)], txt.at[pl.ds(ROWS, ROWS)], gp_sem.at[0], gp_sem.at[1], partner)
    gather_p.start()
    relay = [
        to_row(txt.at[pl.ds(2 * ROWS + k * CHUNK, CHUNK)], txt.at[pl.ds(3 * ROWS + k * CHUNK, CHUNK)], gf_send.at[k], gf_recv.at[k], partner)
        for k in range(STEPS)
    ]

    def logit_block(r0, nr, c0, nc):
        rows = pl.ds(r0, nr)
        cols = pl.ds(c0, nc)
        dots = lax.dot_general(img[rows, :], txt[cols, :], (((1,), (1,)), ((), ())), preferred_element_type=F32)
        e = jnp.exp2(dots * scale2)
        exps[rows, cols] = e
        m = e * dots
        for values, row_sum, col_sum in ((e, row_e, col_e), (m, row_m, col_m)):
            acc = values[:, 0:128]
            for q in range(1, nc // 128):
                acc = acc + values[:, q * 128:(q + 1) * 128]
            row_sum[rows, :] += acc
            col_sum[:, cols] += jnp.sum(values.reshape(nr // 8, 8, nc), axis=0)

    def own_rows(c0):
        def body(i, carry):
            logit_block(pl.multiple_of(i * 512, 512), 512, c0, CHUNK)
            return carry
        lax.fori_loop(0, 2, body, 0)

    def sweep_cols(r0, c0, n):
        if n == 0:
            return
        def body(i, carry):
            logit_block(r0, CHUNK, pl.multiple_of(c0 + i * CHUNK, CHUNK), CHUNK)
            return carry
        lax.fori_loop(0, n, body, 0)

    def sweep_rows(r0, c0, n):
        if n == 0:
            return
        def body(i, carry):
            logit_block(pl.multiple_of(r0 + i * CHUNK, CHUNK), CHUNK, c0, CHUNK)
            return carry
        lax.fori_loop(0, n, body, 0)

    def four_cols(c0):
        def body(i, carry):
            own_rows(pl.multiple_of(c0 + i * CHUNK, CHUNK))
            return carry
        lax.fori_loop(0, STEPS, body, 0)

    four_cols(0)

    def diag_body(i, acc):
        part = pl.ds(pl.multiple_of(i * 128, 128), 128)
        prod = img[part, :].astype(F32) * txt[part, :].astype(F32)
        return acc + jnp.sum(prod.reshape(16, 8, DIM), axis=0)
    diag_sum = jnp.sum(lax.fori_loop(0, 8, diag_body, jnp.zeros((8, DIM), F32)))

    gather_p.wait_recv()
    four_cols(ROWS)
    for k in range(STEPS):
        new_row = ROWS + k * CHUNK
        gather_x[k].wait_recv()
        relay[k].start()
        own_rows(2 * ROWS + k * CHUNK)
        gather_y[k].wait_recv()
        sweep_cols(new_row, 0, 2 * STEPS)
        sweep_cols(new_row, 2 * ROWS, k + 1)
        sweep_rows(ROWS, 2 * ROWS + k * CHUNK, k)
        relay[k].wait_recv()
        own_rows(3 * ROWS + k * CHUNK)
        sweep_cols(new_row, 3 * ROWS, k + 1)
        sweep_rows(ROWS, 3 * ROWS + k * CHUNK, k)

    row_send[...] = jnp.sum(row_e[...].T, axis=0, keepdims=True)
    col_send[...] = jnp.sum(col_e[...], axis=0, keepdims=True)
    swap_row = to_y(row_send, row_recv, row_sem.at[0], row_sem.at[1])
    swap_row.start()
    swap_col = []
    for t, peer in enumerate(peers):
        swap_col.append(to_row(col_send, col_recv.at[t], col_ssem.at[t], col_rsem.at[t], peer))
        swap_col[t].start()
    swap_row.wait_recv()
    row_tot = row_send[...] + jnp.concatenate([row_recv[:, ROWS:], row_recv[:, :ROWS]], axis=1)
    row_a = row_e
    row_a[...] = jnp.broadcast_to(inv_count / row_tot, (128, IMGS)).T
    for t in range(3):
        swap_col[t].wait_recv()
    def slot(ref, s):
        return ref[:, s * ROWS:(s + 1) * ROWS]
    col_tots = []
    for s in range(4):
        tot = (slot(col_send, s) + slot(col_recv.at[0], s ^ 1)) + (slot(col_recv.at[1], s ^ 2) + slot(col_recv.at[2], s ^ 3))
        col_b[:, s * ROWS:(s + 1) * ROWS] = inv_count / tot
        col_tots.append(tot)

    def d_img_chunk(r0):
        rows = pl.ds(r0, CHUNK)
        def body(j, carry):
            for q in range(4):
                cols = pl.ds(pl.multiple_of(j * 512, 512) + q * 128, 128)
                g_row[:, cols] = (exps[rows, cols] * (row_a[rows, :] + col_b[:, cols])).astype(BF16)
            return carry
        lax.fori_loop(0, TXTS // 512, body, 0)
        return jnp.dot(g_row[...], txt[...], preferred_element_type=F32)

    def d_txt_chunk(c0):
        def body(i, carry):
            rows = pl.ds(pl.multiple_of(i * CHUNK, CHUNK), CHUNK)
            for q in range(CHUNK // 128):
                cols = pl.ds(c0 + q * 128, 128)
                g_col[rows, q * 128:(q + 1) * 128] = (exps[rows, cols] * (row_a[rows, :] + col_b[:, cols])).astype(BF16)
            return carry
        lax.fori_loop(0, IMGS // CHUNK, body, 0)
        return lax.dot_general(g_col[...], img[...], (((0,), (0,)), ((), ())), preferred_element_type=F32)

    send_y, send_p, send_x = [], [], []
    for k in range(STEPS):
        part = pl.ds(k * CHUNK, CHUNK)
        d_img_send[part, :] = d_img_chunk(ROWS + k * CHUNK)
        send_y.append(to_y(d_img_send.at[part], d_img_recv.at[part], ry_send.at[k], ry_recv.at[k]))
        send_y[k].start()
        if k >= 2:
            send_p[k - 2].wait_send()
        ring[k % 2] = d_txt_chunk(3 * ROWS + k * CHUNK)
        send_p.append(to_row(ring.at[k % 2], d_txt_x.at[part], rp_send.at[k], rp_recv.at[k], partner))
        send_p[k].start()
        mine = d_txt_chunk(2 * ROWS + k * CHUNK)
        send_p[k].wait_recv()
        d_txt_x[part, :] += mine
        send_x.append(to_row(d_txt_x.at[part], d_txt_recv.at[part], rx_send.at[k], rx_recv.at[k], across))
        send_x[k].start()

    own_r = row_send[:, :ROWS] + row_recv[:, ROWS:]
    loss_part = jnp.sum(jnp.log(own_r) + jnp.log(col_tots[0])) - 2.0 * scale * diag_sum
    dscale_part = scale * (jnp.sum(row_a[...] * row_m[...]) + jnp.sum(jnp.sum(col_m[...], axis=0, keepdims=True) * col_b[...])
                           - 2.0 * inv_count * diag_sum)
    lane = lax.broadcasted_iota(jnp.int32, (8, 128), 1)
    scal[0] = jnp.where(lane == 0, loss_part * inv_count, dscale_part)
    send_s = []
    for t, peer in enumerate(peers):
        send_s.append(to_row(scal.at[0], scal.at[t + 1], sc_ssem.at[t], sc_rsem.at[t], peer))
        send_s[t].start()

    def fix_body(i, carry):
        part = pl.ds(pl.multiple_of(i * 128, 128), 128)
        on_diag = lax.broadcasted_iota(jnp.int32, (128, 128), 0) == lax.broadcasted_iota(jnp.int32, (128, 128), 1)
        term = (2.0 * inv_count) / (row_a[part, :] + col_b[:, part])
        exps[part, part] = exps[part, part] - jnp.where(on_diag, term, 0.0)
        return carry
    lax.fori_loop(0, ROWS // 128, fix_body, 0)

    for k in range(STEPS):
        part = pl.ds(k * CHUNK, CHUNK)
        send_p[STEPS + k - 2].wait_send()
        ring[k % 2] = d_txt_chunk(ROWS + k * CHUNK)
        send_p.append(to_row(ring.at[k % 2], d_txt_p.at[part], rp_send.at[STEPS + k], rp_recv.at[STEPS + k], partner))
        send_p[STEPS + k].start()

    for t in range(3):
        send_s[t].wait_recv()
    scal_y[0] = (scal[0] + scal[1]) + (scal[2] + scal[3])
    swap_s = to_y(scal_y.at[0], scal_y.at[1], sc_ssem.at[3], sc_rsem.at[3])
    swap_s.start()

    outs = []
    for k in range(STEPS):
        part = pl.ds(k * CHUNK, CHUNK)
        slot_k = k % 2
        d_img_own[...] = d_img_chunk(k * CHUNK)
        d_txt_own[...] = d_txt_chunk(k * CHUNK)
        send_p[STEPS + k].wait_recv()
        d_txt_own[...] += d_txt_p[part, :]
        if k >= 2:
            outs[2 * k - 4].wait()
            outs[2 * k - 3].wait()
        send_y[k].wait_recv()
        out_stage[slot_k, 0] = (scale * (d_img_own[...] + d_img_recv[part, :])).astype(BF16)
        outs.append(pltpu.make_async_copy(out_stage.at[slot_k, 0], dimg_hbm.at[part], out_sem.at[2 * k]))
        outs[2 * k].start()
        send_x[k].wait_recv()
        out_stage[slot_k, 1] = (scale * (d_txt_own[...] + d_txt_recv[part, :])).astype(BF16)
        outs.append(pltpu.make_async_copy(out_stage.at[slot_k, 1], dtxt_hbm.at[part], out_sem.at[2 * k + 1]))
        outs[2 * k + 1].start()

    swap_s.wait_recv()
    total = scal_y[0] + scal_y[1]
    loss_ref[0, 0] = total[0, 0]
    dscale_ref[0, 0] = total[0, 1]

    for k in range(STEPS):
        gather_x[k].wait_send()
        gather_y[k].wait_send()
        relay[k].wait_send()
        send_y[k].wait_send()
        send_x[k].wait_send()
    gather_p.wait_send()
    swap_row.wait_send()
    for t in range(3):
        swap_col[t].wait_send()
        send_s[t].wait_send()
    swap_s.wait_send()
    for k in range(2 * STEPS - 2, 2 * STEPS):
        send_p[k].wait_send()
    for k in range(2 * STEPS - 4, 2 * STEPS):
        outs[k].wait()


def solution(mesh):
    batch_spec = P(("row", "col"), None)
    n_dev = mesh.shape["row"] * mesh.shape["col"]
    inv_count = 1.0 / (2 * ROWS * n_dev)
    dma = pltpu.SemaphoreType.DMA

    def local_tile(img_loc, txt_loc, log_scale):
        any_spec = pl.BlockSpec(memory_space=pl.ANY)
        smem_spec = pl.BlockSpec(memory_space=pltpu.SMEM)
        loss, d_img, d_txt, d_scale = pl.pallas_call(
            functools.partial(kernel, inv_count),
            out_shape=(
                jax.ShapeDtypeStruct((1, 1), F32),
                jax.ShapeDtypeStruct((ROWS, DIM), BF16),
                jax.ShapeDtypeStruct((ROWS, DIM), BF16),
                jax.ShapeDtypeStruct((1, 1), F32),
            ),
            in_specs=[smem_spec, any_spec, any_spec],
            out_specs=(smem_spec, any_spec, any_spec, smem_spec),
            scratch_shapes=[
                pltpu.VMEM((IMGS, DIM), BF16),
                pltpu.VMEM((TXTS, DIM), BF16),
                pltpu.VMEM((IMGS, TXTS), F32),
                pltpu.VMEM((IMGS, 128), F32),
                pltpu.VMEM((IMGS, 128), F32),
                pltpu.VMEM((8, TXTS), F32),
                pltpu.VMEM((8, TXTS), F32),
                pltpu.VMEM((1, IMGS), F32),
                pltpu.VMEM((1, IMGS), F32),
                pltpu.VMEM((1, TXTS), F32),
                pltpu.VMEM((3, 1, TXTS), F32),
                pltpu.VMEM((1, TXTS), F32),
                pltpu.VMEM((CHUNK, TXTS), BF16),
                pltpu.VMEM((IMGS, CHUNK), BF16),
                pltpu.VMEM((ROWS, DIM), F32),
                pltpu.VMEM((ROWS, DIM), F32),
                pltpu.VMEM((CHUNK, DIM), F32),
                pltpu.VMEM((2, CHUNK, DIM), F32),
                pltpu.VMEM((ROWS, DIM), F32),
                pltpu.VMEM((ROWS, DIM), F32),
                pltpu.VMEM((ROWS, DIM), F32),
                pltpu.VMEM((CHUNK, DIM), F32),
                pltpu.VMEM((2, 2, CHUNK, DIM), BF16),
                pltpu.VMEM((4, 8, 128), F32),
                pltpu.VMEM((2, 8, 128), F32),
                dma((2,)),
                dma((STEPS,)), dma((STEPS,)),
                dma((STEPS,)), dma((STEPS,)),
                dma((2,)),
                dma((STEPS,)), dma((STEPS,)),
                dma((2,)),
                dma((3,)), dma((3,)),
                dma((STEPS,)), dma((STEPS,)),
                dma((2 * STEPS,)), dma((2 * STEPS,)),
                dma((STEPS,)), dma((STEPS,)),
                dma((4,)), dma((4,)),
                dma((2 * STEPS,)),
            ],
            compiler_params=pltpu.CompilerParams(
                collective_id=0, has_side_effects=True, vmem_limit_bytes=67043328,
            ),
            name="clip_loss",
        )(log_scale.reshape(1, 1), img_loc, txt_loc)
        return loss.reshape(()), d_img, d_txt, d_scale.reshape(())

    return jax.shard_map(local_tile, mesh=mesh, in_specs=(batch_spec, batch_spec, P()), out_specs=(P(), batch_spec, batch_spec, P()), check_vma=False)
```

time: 309 us -> 115 us (0.37)
  waiting for transfers between devices: 124 us -> 0 us
  Pallas kernels: 0 us -> 107 us
  blocking collectives: 54.3 us -> 0 us
  other arithmetic: 43.1 us -> 0 us
  matrix products: 42.5 us -> 0 us
  local copies, waits for them, and re-layouts: 27.2 us -> 3.32 us
  between operations: 16.3 us -> 4.72 us
    pallas_call x0 -> x1, Pallas kernels: none -> 107 us  [local_tile(): pl.pallas_call(functools.partial(kernel, inv_count), out_shape=(jax.Shape...]
    all_gather x2 -> x0, waiting for transfers between devices: 66.1 us -> none  [the longest x1 33.1 us: local_tile(): img_block = lax.all_gather(img_loc, 'col', tiled=True)]
    reduce_scatter x2 -> x0, waiting for transfers between devices: 56.9 us -> none  [the longest x1 56.9 us: local_tile(): txt_sum = lax.psum_scatter(txt_part, 'row', scatter_dimension=0, tiled=True)]
    dot_general x3 -> x0, matrix products: 42.5 us -> none  [the longest x1 17.8 us: local_tile(): jnp.einsum('id,jd->ij', img_block, txt_block, preferred_element_type=jnp....]
    psum x3 -> x0, blocking collectives: 39.1 us -> none  [the longest x1 24 us: local_tile(): total_loss = lax.psum(loss_part, both_axes) * inv_count]
    convert_element_type x3 -> x0, other arithmetic: 26.9 us -> none  [the longest x1 21.2 us: local_tile(): grad_bf = grad_tile.astype(jnp.bfloat16)]
    gather x1 -> x0, local copies, waits for them, and re-layouts: 16.6 us -> none  [local_tile(): own_diag = jnp.diagonal(own_block)]
    reduce_sum x2 -> x0, other arithmetic: 16.1 us -> none  [the longest x1 15.5 us: local_tile(): row_part = jnp.sum(row_exp, axis=1)]
  transfers between devices with their start and end apart: 4 -> 0, of which waited for: 3 -> 0; matrix products, arithmetic and copies ran while one was open for 13% -> 0% of each run, Pallas kernels for 0% -> 0%
where the time goes in v1:
time: 115 us
  Pallas kernels  107 us (93%)
  between operations  4.72 us (4%)
  local copies, waits for them, and re-layouts  3.32 us (3%)
    pallas_call x1, Pallas kernels, local_tile(): pl.pallas_call(functools.partial(kernel, inv_count), out_shape=(jax.Shape...  107 us
    unnamed x4, local copies, waits for them, and re-layouts  3.32 us

profile of v1, /device:TPU:0, one launch (start us, length us, event | category | flops | bytes accessed | tf_op | source)
XLA Modules:
  0.0 115.2 jit_solution(8377477770703877791)
XLA Ops:
  1.3 107.2 %clip_loss.1 = (f32[1,1]{1,0:T(1,128)}, bf16[1024,512]{1,0:T(8,128)(2,1)}, bf16[1024,512]{1,0:T(8,128)(2,1)}, f32[1,1]{1,0:T(1,128)}) custom-call(f32[1,1]{1,0:T(1,128)} %bitcast.3.scale_ref, bf16[1024,512]{1,0:T(8,128)(2,1)} %img_hbm.1, bf16[1024,512]{1,0:T(8,128)(2,1)} %txt_hbm.1), custom_call_target="tpu_custom_call" | custom-call | tf_op jit(solution)/shard_map/clip_loss/pallas_call | solution.py:287
  109.1 0.0 copy-start
  109.1 2.4 %copy.13 = bf16[1024,512]{1,0:T(8,128)(2,1)} copy(bf16[1024,512]{1,0:T(8,128)(2,1)} %get-tuple-element.17) | data formatting | bytes 2097152
  111.5 0.0 copy-done
  111.5 1.0 copy.14
Async XLA Ops:
  109.1 2.4 %copy-start = (bf16[1024,512]{1,0:T(8,128)(2,1)S(1)}, bf16[1024,512]{1,0:T(8,128)(2,1)}, u32[]{:S(2)}) copy-start(bf16[1024,512]{1,0:T(8,128)(2,1)} %get-tuple-element.18) | copy-start | bytes 3145732

commit v2 on v1

--- a/solution.py
+++ b/solution.py
@@ -17,12 +17,13 @@
 STEPS = ROWS // CHUNK
 IMGS = 2 * ROWS
 TXTS = 4 * ROWS
+X_BASE = 2 * ROWS
 LOG2E = math.log2(math.e)
 
 
 def kernel(inv_count, scale_ref, img_hbm, txt_hbm, loss_ref, dimg_hbm, dtxt_hbm, dscale_ref,
            img, txt, exps, row_e, row_m, col_e, col_m, row_send, row_recv, col_send, col_recv, col_b,
-           g_row, g_col, d_img_send, d_img_recv, d_img_own, ring, d_txt_x, d_txt_p, d_txt_recv, d_txt_own, out_stage,
+           d_img_send, d_img_recv, d_img_own, ring, d_txt_x, d_txt_p, d_txt_recv, out_stage,
            scal, scal_y, load_sem, gy_send, gy_recv, gx_send, gx_recv, gp_sem, gf_send, gf_recv, row_sem, col_ssem, col_rsem,
            ry_send, ry_recv, rp_send, rp_recv, rx_send, rx_recv, sc_ssem, sc_rsem, out_sem):
     row = lax.axis_index("row")
@@ -64,14 +65,14 @@
     gather_y, gather_x = [], []
     for k in range(STEPS):
         part = pl.ds(k * CHUNK, CHUNK)
-        gather_x.append(to_row(txt.at[part], txt.at[pl.ds(2 * ROWS + k * CHUNK, CHUNK)], gx_send.at[k], gx_recv.at[k], across))
+        gather_x.append(to_row(txt.at[part], txt.at[pl.ds(X_BASE + 2 * k * CHUNK, CHUNK)], gx_send.at[k], gx_recv.at[k], across))
         gather_y.append(to_y(img.at[part], img.at[pl.ds(ROWS + k * CHUNK, CHUNK)], gy_send.at[k], gy_recv.at[k]))
         gather_x[k].start()
         gather_y[k].start()
     gather_p = to_row(txt.at[pl.ds(0, ROWS)], txt.at[pl.ds(ROWS, ROWS)], gp_sem.at[0], gp_sem.at[1], partner)
     gather_p.start()
     relay = [
-        to_row(txt.at[pl.ds(2 * ROWS + k * CHUNK, CHUNK)], txt.at[pl.ds(3 * ROWS + k * CHUNK, CHUNK)], gf_send.at[k], gf_recv.at[k], partner)
+        to_row(txt.at[pl.ds(X_BASE + 2 * k * CHUNK, CHUNK)], txt.at[pl.ds(X_BASE + (2 * k + 1) * CHUNK, CHUNK)], gf_send.at[k], gf_recv.at[k], partner)
         for k in range(STEPS)
     ]
 
@@ -89,35 +90,11 @@
             row_sum[rows, :] += acc
             col_sum[:, cols] += jnp.sum(values.reshape(nr // 8, 8, nc), axis=0)
 
-    def own_rows(c0):
-        def body(i, carry):
-            logit_block(pl.multiple_of(i * 512, 512), 512, c0, CHUNK)
-            return carry
-        lax.fori_loop(0, 2, body, 0)
-
-    def sweep_cols(r0, c0, n):
-        if n == 0:
-            return
-        def body(i, carry):
-            logit_block(r0, CHUNK, pl.multiple_of(c0 + i * CHUNK, CHUNK), CHUNK)
-            return carry
-        lax.fori_loop(0, n, body, 0)
-
-    def sweep_rows(r0, c0, n):
-        if n == 0:
-            return
-        def body(i, carry):
-            logit_block(pl.multiple_of(r0 + i * CHUNK, CHUNK), CHUNK, c0, CHUNK)
-            return carry
-        lax.fori_loop(0, n, body, 0)
-
-    def four_cols(c0):
-        def body(i, carry):
-            own_rows(pl.multiple_of(c0 + i * CHUNK, CHUNK))
-            return carry
-        lax.fori_loop(0, STEPS, body, 0)
-
-    four_cols(0)
+    def own_by_own(i, carry):
+        logit_block(0, ROWS, pl.multiple_of(i * 512, 512), 512)
+        return carry
+
+    lax.fori_loop(0, 2, own_by_own, 0)
 
     def diag_body(i, acc):
         part = pl.ds(pl.multiple_of(i * 128, 128), 128)
@@ -126,20 +103,19 @@
     diag_sum = jnp.sum(lax.fori_loop(0, 8, diag_body, jnp.zeros((8, DIM), F32)))
 
     gather_p.wait_recv()
-    four_cols(ROWS)
+    lax.fori_loop(2, 4, own_by_own, 0)
     for k in range(STEPS):
         new_row = ROWS + k * CHUNK
         gather_x[k].wait_recv()
         relay[k].start()
-        own_rows(2 * ROWS + k * CHUNK)
         gather_y[k].wait_recv()
-        sweep_cols(new_row, 0, 2 * STEPS)
-        sweep_cols(new_row, 2 * ROWS, k + 1)
-        sweep_rows(ROWS, 2 * ROWS + k * CHUNK, k)
+        def new_by_held(i, carry, new_row=new_row):
+            logit_block(new_row, CHUNK, pl.multiple_of(i * 512, 512), 512)
+            return carry
+        lax.fori_loop(0, 4 + k, new_by_held, 0)
         relay[k].wait_recv()
-        own_rows(3 * ROWS + k * CHUNK)
-        sweep_cols(new_row, 3 * ROWS, k + 1)
-        sweep_rows(ROWS, 3 * ROWS + k * CHUNK, k)
+        logit_block(0, ROWS, X_BASE + 2 * k * CHUNK, 2 * CHUNK)
+        logit_block(ROWS, (k + 1) * CHUNK, X_BASE + 2 * k * CHUNK, 2 * CHUNK)
 
     row_send[...] = jnp.sum(row_e[...].T, axis=0, keepdims=True)
     col_send[...] = jnp.sum(col_e[...], axis=0, keepdims=True)
@@ -156,60 +132,86 @@
     for t in range(3):
         swap_col[t].wait_recv()
     def slot(ref, s):
-        return ref[:, s * ROWS:(s + 1) * ROWS]
-    col_tots = []
+        if s < 2:
+            return ref[:, s * ROWS:(s + 1) * ROWS]
+        starts = [X_BASE + (2 * k + s - 2) * CHUNK for k in range(STEPS)]
+        return jnp.concatenate([ref[:, c:c + CHUNK] for c in starts], axis=1)
     for s in range(4):
         tot = (slot(col_send, s) + slot(col_recv.at[0], s ^ 1)) + (slot(col_recv.at[1], s ^ 2) + slot(col_recv.at[2], s ^ 3))
-        col_b[:, s * ROWS:(s + 1) * ROWS] = inv_count / tot
-        col_tots.append(tot)
+        if s < 2:
+            col_b[:, s * ROWS:(s + 1) * ROWS] = inv_count / tot
+        else:
+            for k in range(STEPS):
+                start = X_BASE + (2 * k + s - 2) * CHUNK
+                col_b[:, start:start + CHUNK] = inv_count / tot[:, k * CHUNK:(k + 1) * CHUNK]
 
     def d_img_chunk(r0):
         rows = pl.ds(r0, CHUNK)
-        def body(j, carry):
-            for q in range(4):
-                cols = pl.ds(pl.multiple_of(j * 512, 512) + q * 128, 128)
-                g_row[:, cols] = (exps[rows, cols] * (row_a[rows, :] + col_b[:, cols])).astype(BF16)
-            return carry
-        lax.fori_loop(0, TXTS // 512, body, 0)
-        return jnp.dot(g_row[...], txt[...], preferred_element_type=F32)
+        total = None
+        for j in range(TXTS // 512):
+            g = [exps[rows, c:c + 128] * (row_a[rows, :] + col_b[:, c:c + 128]) for c in range(j * 512, (j + 1) * 512, 128)]
+            g = jnp.concatenate([v.astype(BF16) for v in g], axis=1)
+            part = jnp.dot(g, txt[j * 512:(j + 1) * 512, :], preferred_element_type=F32)
+            total = part if total is None else total + part
+        return total
 
     def d_txt_chunk(c0):
-        def body(i, carry):
-            rows = pl.ds(pl.multiple_of(i * CHUNK, CHUNK), CHUNK)
+        total = None
+        for i in range(IMGS // 512):
+            rows = slice(i * 512, (i + 1) * 512)
+            g = []
             for q in range(CHUNK // 128):
                 cols = pl.ds(c0 + q * 128, 128)
-                g_col[rows, q * 128:(q + 1) * 128] = (exps[rows, cols] * (row_a[rows, :] + col_b[:, cols])).astype(BF16)
-            return carry
-        lax.fori_loop(0, IMGS // CHUNK, body, 0)
-        return lax.dot_general(g_col[...], img[...], (((0,), (0,)), ((), ())), preferred_element_type=F32)
-
-    send_y, send_p, send_x = [], [], []
-    for k in range(STEPS):
-        part = pl.ds(k * CHUNK, CHUNK)
-        d_img_send[part, :] = d_img_chunk(ROWS + k * CHUNK)
-        send_y.append(to_y(d_img_send.at[part], d_img_recv.at[part], ry_send.at[k], ry_recv.at[k]))
-        send_y[k].start()
-        if k >= 2:
-            send_p[k - 2].wait_send()
-        ring[k % 2] = d_txt_chunk(3 * ROWS + k * CHUNK)
-        send_p.append(to_row(ring.at[k % 2], d_txt_x.at[part], rp_send.at[k], rp_recv.at[k], partner))
-        send_p[k].start()
-        mine = d_txt_chunk(2 * ROWS + k * CHUNK)
-        send_p[k].wait_recv()
+                g.append((exps[rows, cols] * (row_a[rows, :] + col_b[:, cols])).astype(BF16))
+            g = jnp.concatenate(g, axis=1)
+            part = lax.dot_general(g, img[rows, :], (((0,), (0,)), ((), ())), preferred_element_type=F32)
+            total = part if total is None else total + part
+        return total
+
+    def chunk_of(k):
+        return pl.ds(pl.multiple_of(k * CHUNK, CHUNK), CHUNK)
+
+    def send_y(k):
+        part = chunk_of(k)
+        return to_y(d_img_send.at[part], d_img_recv.at[part], ry_send.at[k], ry_recv.at[k])
+
+    def send_x(k):
+        part = chunk_of(k)
+        return to_row(d_txt_x.at[part], d_txt_recv.at[part], rx_send.at[k], rx_recv.at[k], across)
+
+    def send_p(k, half, dst):
+        n = half * STEPS + k
+        return to_row(ring.at[lax.rem(k, 2)], dst.at[chunk_of(k)], rp_send.at[n], rp_recv.at[n], partner)
+
+    send_s = [to_row(scal.at[0], scal.at[t + 1], sc_ssem.at[t], sc_rsem.at[t], peer) for t, peer in enumerate(peers)]
+
+    def far_body(k, carry):
+        part = chunk_of(k)
+        x_cols = pl.multiple_of(X_BASE + 2 * k * CHUNK, CHUNK)
+        @pl.when(k >= 2)
+        def _():
+            send_p(k - 2, 0, d_txt_x).wait_send()
+        ring[lax.rem(k, 2)] = d_txt_chunk(x_cols + CHUNK)
+        send_p(k, 0, d_txt_x).start()
+        d_img_send[part, :] = d_img_chunk(pl.multiple_of(ROWS + k * CHUNK, CHUNK))
+        send_y(k).start()
+        mine = d_txt_chunk(x_cols)
+        send_p(k, 0, d_txt_x).wait_recv()
         d_txt_x[part, :] += mine
-        send_x.append(to_row(d_txt_x.at[part], d_txt_recv.at[part], rx_send.at[k], rx_recv.at[k], across))
-        send_x[k].start()
-
-    own_r = row_send[:, :ROWS] + row_recv[:, ROWS:]
-    loss_part = jnp.sum(jnp.log(own_r) + jnp.log(col_tots[0])) - 2.0 * scale * diag_sum
-    dscale_part = scale * (jnp.sum(row_a[...] * row_m[...]) + jnp.sum(jnp.sum(col_m[...], axis=0, keepdims=True) * col_b[...])
-                           - 2.0 * inv_count * diag_sum)
-    lane = lax.broadcasted_iota(jnp.int32, (8, 128), 1)
-    scal[0] = jnp.where(lane == 0, loss_part * inv_count, dscale_part)
-    send_s = []
-    for t, peer in enumerate(peers):
-        send_s.append(to_row(scal.at[0], scal.at[t + 1], sc_ssem.at[t], sc_rsem.at[t], peer))
-        send_s[t].start()
+        send_x(k).start()
+
+        @pl.when(k == 0)
+        def _():
+            own_r = row_send[:, :ROWS] + row_recv[:, ROWS:]
+            loss_part = jnp.sum(jnp.log(own_r) - jnp.log(col_b[:, :ROWS] / inv_count)) - 2.0 * scale * diag_sum
+            dscale_part = scale * (jnp.sum(row_a[...] * row_m[...]) + jnp.sum(jnp.sum(col_m[...], axis=0, keepdims=True) * col_b[...])
+                                   - 2.0 * inv_count * diag_sum)
+            lane = lax.broadcasted_iota(jnp.int32, (8, 128), 1)
+            scal[0] = jnp.where(lane == 0, loss_part * inv_count, dscale_part)
+            for t in range(3):
+                send_s[t].start()
+        return carry
+    lax.fori_loop(0, STEPS, far_body, 0)
 
     def fix_body(i, carry):
         part = pl.ds(pl.multiple_of(i * 128, 128), 128)
@@ -219,12 +221,22 @@
         return carry
     lax.fori_loop(0, ROWS // 128, fix_body, 0)
 
-    for k in range(STEPS):
-        part = pl.ds(k * CHUNK, CHUNK)
-        send_p[STEPS + k - 2].wait_send()
-        ring[k % 2] = d_txt_chunk(ROWS + k * CHUNK)
-        send_p.append(to_row(ring.at[k % 2], d_txt_p.at[part], rp_send.at[STEPS + k], rp_recv.at[STEPS + k], partner))
-        send_p[STEPS + k].start()
+    def near_body(k, carry):
+        part = chunk_of(k)
+        @pl.when(k < 2)
+        def _():
+            send_p(k + 2, 0, d_txt_x).wait_send()
+        @pl.when(k >= 2)
+        def _():
+            send_p(k - 2, 1, d_txt_p).wait_send()
+        ring[lax.rem(k, 2)] = d_txt_chunk(pl.multiple_of(ROWS + k * CHUNK, CHUNK))
+        send_p(k, 1, d_txt_p).start()
+        d_img_own[part, :] = d_img_chunk(pl.multiple_of(k * CHUNK, CHUNK))
+        mine = d_txt_chunk(pl.multiple_of(k * CHUNK, CHUNK))
+        send_p(k, 1, d_txt_p).wait_recv()
+        d_txt_p[part, :] += mine
+        return carry
+    lax.fori_loop(0, STEPS, near_body, 0)
 
     for t in range(3):
         send_s[t].wait_recv()
@@ -236,19 +248,15 @@
     for k in range(STEPS):
         part = pl.ds(k * CHUNK, CHUNK)
         slot_k = k % 2
-        d_img_own[...] = d_img_chunk(k * CHUNK)
-        d_txt_own[...] = d_txt_chunk(k * CHUNK)
-        send_p[STEPS + k].wait_recv()
-        d_txt_own[...] += d_txt_p[part, :]
         if k >= 2:
             outs[2 * k - 4].wait()
             outs[2 * k - 3].wait()
-        send_y[k].wait_recv()
-        out_stage[slot_k, 0] = (scale * (d_img_own[...] + d_img_recv[part, :])).astype(BF16)
+        send_y(k).wait_recv()
+        out_stage[slot_k, 0] = (scale * (d_img_own[part, :] + d_img_recv[part, :])).astype(BF16)
         outs.append(pltpu.make_async_copy(out_stage.at[slot_k, 0], dimg_hbm.at[part], out_sem.at[2 * k]))
         outs[2 * k].start()
-        send_x[k].wait_recv()
-        out_stage[slot_k, 1] = (scale * (d_txt_own[...] + d_txt_recv[part, :])).astype(BF16)
+        send_x(k).wait_recv()
+        out_stage[slot_k, 1] = (scale * (d_txt_p[part, :] + d_txt_recv[part, :])).astype(BF16)
         outs.append(pltpu.make_async_copy(out_stage.at[slot_k, 1], dtxt_hbm.at[part], out_sem.at[2 * k + 1]))
         outs[2 * k + 1].start()
 
@@ -261,16 +269,16 @@
         gather_x[k].wait_send()
         gather_y[k].wait_send()
         relay[k].wait_send()
-        send_y[k].wait_send()
-        send_x[k].wait_send()
+        send_y(k).wait_send()
+        send_x(k).wait_send()
     gather_p.wait_send()
     swap_row.wait_send()
     for t in range(3):
         swap_col[t].wait_send()
         send_s[t].wait_send()
     swap_s.wait_send()
-    for k in range(2 * STEPS - 2, 2 * STEPS):
-        send_p[k].wait_send()
+    for k in range(STEPS - 2, STEPS):
+        send_p(k, 1, d_txt_p).wait_send()
     for k in range(2 * STEPS - 4, 2 * STEPS):
         outs[k].wait()
 
@@ -307,16 +315,13 @@
                 pltpu.VMEM((1, TXTS), F32),
                 pltpu.VMEM((3, 1, TXTS), F32),
                 pltpu.VMEM((1, TXTS), F32),
-                pltpu.VMEM((CHUNK, TXTS), BF16),
-                pltpu.VMEM((IMGS, CHUNK), BF16),
-                pltpu.VMEM((ROWS, DIM), F32),
-                pltpu.VMEM((ROWS, DIM), F32),
-                pltpu.VMEM((CHUNK, DIM), F32),
+                pltpu.VMEM((ROWS, DIM), F32),
+                pltpu.VMEM((ROWS, DIM), F32),
+                pltpu.VMEM((ROWS, DIM), F32),
                 pltpu.VMEM((2, CHUNK, DIM), F32),
                 pltpu.VMEM((ROWS, DIM), F32),
                 pltpu.VMEM((ROWS, DIM), F32),
                 pltpu.VMEM((ROWS, DIM), F32),
-                pltpu.VMEM((CHUNK, DIM), F32),
                 pltpu.VMEM((2, 2, CHUNK, DIM), BF16),
                 pltpu.VMEM((4, 8, 128), F32),
                 pltpu.VMEM((2, 8, 128), F32),

time: 115 us -> 96 us (0.83)
  Pallas kernels: 107 us -> 87.8 us
    pallas_call x1, Pallas kernels: 107 us -> 87.8 us  [local_tile(): pl.pallas_call(functools.partial(kernel, inv_count), out_shape=(jax.Shape...]
where the time goes in v2:
time: 96 us; the launch traced here: 95.8 us
  Pallas kernels  87.8 us (91%)
  between operations  4.72 us (5%)
  local copies, waits for them, and re-layouts  3.32 us (3%)
    pallas_call x1, Pallas kernels, local_tile(): pl.pallas_call(functools.partial(kernel, inv_count), out_shape=(jax.Shape...  87.8 us
    unnamed x4, local copies, waits for them, and re-layouts  3.32 us

profile of v2, /device:TPU:0, one launch (start us, length us, event | category | flops | bytes accessed | tf_op | source)
XLA Modules:
  0.0 95.8 jit_solution(3391296456913926700)
XLA Ops:
  1.3 87.8 %clip_loss.1 = (f32[1,1]{1,0:T(1,128)}, bf16[1024,512]{1,0:T(8,128)(2,1)}, bf16[1024,512]{1,0:T(8,128)(2,1)}, f32[1,1]{1,0:T(1,128)}) custom-call(f32[1,1]{1,0:T(1,128)} %bitcast.3.scale_ref, bf16[1024,512]{1,0:T(8,128)(2,1)} %img_hbm.1, bf16[1024,512]{1,0:T(8,128)(2,1)} %txt_hbm.1), custom_call_target="tpu_custom_call" | custom-call | tf_op jit(solution)/shard_map/clip_loss/pallas_call | solution.py:295
  89.7 0.0 copy-start
  89.7 2.4 %copy.13 = bf16[1024,512]{1,0:T(8,128)(2,1)} copy(bf16[1024,512]{1,0:T(8,128)(2,1)} %get-tuple-element.17) | data formatting | bytes 2097152
  92.0 0.0 copy-done
  92.0 1.0 %copy.14 = bf16[1024,512]{1,0:T(8,128)(2,1)} copy(bf16[1024,512]{1,0:T(8,128)(2,1)S(1)} %copy-done) | data formatting | bytes 2097152
Async XLA Ops:
  89.7 2.4 %copy-start = (bf16[1024,512]{1,0:T(8,128)(2,1)S(1)}, bf16[1024,512]{1,0:T(8,128)(2,1)}, u32[]{:S(2)}) copy-start(bf16[1024,512]{1,0:T(8,128)(2,1)} %get-tuple-element.18) | copy-start | bytes 3145732

commit v3 on v2

--- a/solution.py
+++ b/solution.py
@@ -9,23 +9,28 @@
 from jax.sharding import PartitionSpec as P
 
 MESH = pl.DeviceIdType.MESH
+VMEM_LIMIT = 61 * 1024 * 1024
 F32 = jnp.float32
 BF16 = jnp.bfloat16
 ROWS = 1024
 DIM = 512
 CHUNK = 256
 STEPS = ROWS // CHUNK
+PIECE = 128
+GATHER = (2, 2, 2, 1, 1)
+G_START = tuple(sum(GATHER[:k]) for k in range(len(GATHER)))
+G_STEPS = len(GATHER)
 IMGS = 2 * ROWS
 TXTS = 4 * ROWS
 X_BASE = 2 * ROWS
 LOG2E = math.log2(math.e)
 
 
-def kernel(inv_count, scale_ref, img_hbm, txt_hbm, loss_ref, dimg_hbm, dtxt_hbm, dscale_ref,
-           img, txt, exps, row_e, row_m, col_e, col_m, row_send, row_recv, col_send, col_recv, col_b,
-           d_img_send, d_img_recv, d_img_own, ring, d_txt_x, d_txt_p, d_txt_recv, out_stage,
+def kernel(inv_count, scale_ref, img_hbm, txt_hbm, loss_ref, dimg_ref, dtxt_ref, dscale_ref,
+           img, txt, far, txt_t, exps, row_e, row_m, col_e, col_m, row_send, row_recv, col_send, col_recv, col_b,
+           d_img_send, d_img_recv, d_img_own, ring, d_txt_x, d_txt_p, d_txt_recv,
            scal, scal_y, load_sem, gy_send, gy_recv, gx_send, gx_recv, gp_sem, gf_send, gf_recv, row_sem, col_ssem, col_rsem,
-           ry_send, ry_recv, rp_send, rp_recv, rx_send, rx_recv, sc_ssem, sc_rsem, out_sem):
+           ry_send, ry_recv, rp_send, rp_recv, rx_send, rx_recv, sc_ssem, sc_rsem):
     row = lax.axis_index("row")
     col = lax.axis_index("col")
     core = lax.rem(row, 2)
@@ -42,7 +47,8 @@
         return pltpu.make_async_remote_copy(src, dst, ssem, rsem, device_id={"row": peer, "col": col}, device_id_type=MESH)
 
     load_img = pltpu.make_async_copy(img_hbm, img.at[pl.ds(0, ROWS)], load_sem.at[0])
-    load_txt = pltpu.make_async_copy(txt_hbm, txt.at[pl.ds(0, ROWS)], load_sem.at[1])
+    load_txt = pltpu.make_async_copy(txt_hbm, txt.at[0], load_sem.at[1])
+    txt_pieces = txt.at[0].reshape(ROWS // PIECE, PIECE, DIM)
     load_img.start()
     load_txt.start()
 
@@ -62,24 +68,22 @@
     load_txt.wait()
     pl.semaphore_wait(barrier, 4)
 
-    gather_y, gather_x = [], []
-    for k in range(STEPS):
-        part = pl.ds(k * CHUNK, CHUNK)
-        gather_x.append(to_row(txt.at[part], txt.at[pl.ds(X_BASE + 2 * k * CHUNK, CHUNK)], gx_send.at[k], gx_recv.at[k], across))
-        gather_y.append(to_y(img.at[part], img.at[pl.ds(ROWS + k * CHUNK, CHUNK)], gy_send.at[k], gy_recv.at[k]))
+    gather_y, gather_x, relay = [], [], []
+    for k in range(G_STEPS):
+        pieces = pl.ds(G_START[k], GATHER[k])
+        part = pl.ds(G_START[k] * PIECE, GATHER[k] * PIECE)
+        gather_x.append(to_row(txt_pieces.at[pieces], far.at[pieces, 0], gx_send.at[k], gx_recv.at[k], across))
+        gather_y.append(to_y(img.at[part], img.at[pl.ds(ROWS + G_START[k] * PIECE, GATHER[k] * PIECE)], gy_send.at[k], gy_recv.at[k]))
+        relay.append(to_row(far.at[pieces, 0], far.at[pieces, 1], gf_send.at[k], gf_recv.at[k], partner))
         gather_x[k].start()
         gather_y[k].start()
-    gather_p = to_row(txt.at[pl.ds(0, ROWS)], txt.at[pl.ds(ROWS, ROWS)], gp_sem.at[0], gp_sem.at[1], partner)
+    gather_p = to_row(txt.at[0], txt.at[1], gp_sem.at[0], gp_sem.at[1], partner)
     gather_p.start()
-    relay = [
-        to_row(txt.at[pl.ds(X_BASE + 2 * k * CHUNK, CHUNK)], txt.at[pl.ds(X_BASE + (2 * k + 1) * CHUNK, CHUNK)], gf_send.at[k], gf_recv.at[k], partner)
-        for k in range(STEPS)
-    ]
-
-    def logit_block(r0, nr, c0, nc):
+
+    def logit_block(r0, nr, c0, nc, texts, on_rows):
         rows = pl.ds(r0, nr)
         cols = pl.ds(c0, nc)
-        dots = lax.dot_general(img[rows, :], txt[cols, :], (((1,), (1,)), ((), ())), preferred_element_type=F32)
+        dots = lax.dot_general(img[rows, :], texts, (((1,), (1 if on_rows else 0,)), ((), ())), preferred_element_type=F32)
         e = jnp.exp2(dots * scale2)
         exps[rows, cols] = e
         m = e * dots
@@ -90,32 +94,55 @@
             row_sum[rows, :] += acc
             col_sum[:, cols] += jnp.sum(values.reshape(nr // 8, 8, nc), axis=0)
 
-    def own_by_own(i, carry):
-        logit_block(0, ROWS, pl.multiple_of(i * 512, 512), 512)
-        return carry
-
-    lax.fori_loop(0, 2, own_by_own, 0)
+    def own_by_held(slot):
+        def body(i, carry):
+            part = pl.ds(pl.multiple_of(i * 512, 512), 512)
+            logit_block(0, ROWS, pl.multiple_of(slot * ROWS + i * 512, 512), 512, txt[slot, part, :], True)
+            return carry
+        lax.fori_loop(0, 2, body, 0)
+
+    def turn_held(slot):
+        def body(i, carry):
+            part = pl.ds(pl.multiple_of(i * CHUNK, CHUNK), CHUNK)
+            txt_t[:, pl.ds(pl.multiple_of(slot * ROWS + i * CHUNK, CHUNK), CHUNK)] = txt[slot, part, :].T
+            return carry
+        lax.fori_loop(0, STEPS, body, 0)
+
+    own_by_held(0)
+    turn_held(0)
 
     def diag_body(i, acc):
         part = pl.ds(pl.multiple_of(i * 128, 128), 128)
-        prod = img[part, :].astype(F32) * txt[part, :].astype(F32)
+        prod = img[part, :].astype(F32) * txt[0, part, :].astype(F32)
         return acc + jnp.sum(prod.reshape(16, 8, DIM), axis=0)
     diag_sum = jnp.sum(lax.fori_loop(0, 8, diag_body, jnp.zeros((8, DIM), F32)))
 
     gather_p.wait_recv()
-    lax.fori_loop(2, 4, own_by_own, 0)
-    for k in range(STEPS):
-        new_row = ROWS + k * CHUNK
+    own_by_held(1)
+    turn_held(1)
+    for k in range(G_STEPS):
+        n_rows = GATHER[k] * PIECE
+        done = G_START[k] * PIECE
+        new_row = ROWS + done
         gather_x[k].wait_recv()
         relay[k].start()
         gather_y[k].wait_recv()
-        def new_by_held(i, carry, new_row=new_row):
-            logit_block(new_row, CHUNK, pl.multiple_of(i * 512, 512), 512)
+        def new_by_held(i, carry, new_row=new_row, n_rows=n_rows):
+            c0 = pl.multiple_of(i * 1024, 1024)
+            logit_block(new_row, n_rows, c0, 1024, txt_t[:, pl.ds(c0, 1024)], False)
             return carry
-        lax.fori_loop(0, 4 + k, new_by_held, 0)
+        n_held = X_BASE + 2 * done
+        lax.fori_loop(0, n_held // 1024, new_by_held, 0)
+        if n_held % 1024:
+            c0 = n_held // 1024 * 1024
+            logit_block(new_row, n_rows, c0, n_held - c0, txt_t[:, c0:n_held], False)
         relay[k].wait_recv()
-        logit_block(0, ROWS, X_BASE + 2 * k * CHUNK, 2 * CHUNK)
-        logit_block(ROWS, (k + 1) * CHUNK, X_BASE + 2 * k * CHUNK, 2 * CHUNK)
+        new_cols = 2 * n_rows
+        logit_block(0, new_row + n_rows, n_held, new_cols, far[G_START[k]:G_START[k] + GATHER[k]].reshape(new_cols, DIM), True)
+        if k + 1 < G_STEPS:
+            for p in range(G_START[k], G_START[k] + GATHER[k]):
+                c0 = X_BASE + 2 * p * PIECE
+                txt_t[:, c0:c0 + 2 * PIECE] = far[p].reshape(2 * PIECE, DIM).T
 
     row_send[...] = jnp.sum(row_e[...].T, axis=0, keepdims=True)
     col_send[...] = jnp.sum(col_e[...], axis=0, keepdims=True)
@@ -134,16 +161,17 @@
     def slot(ref, s):
         if s < 2:
             return ref[:, s * ROWS:(s + 1) * ROWS]
-        starts = [X_BASE + (2 * k + s - 2) * CHUNK for k in range(STEPS)]
-        return jnp.concatenate([ref[:, c:c + CHUNK] for c in starts], axis=1)
+        starts = [X_BASE + (2 * p + s - 2) * PIECE for p in range(ROWS // PIECE)]
+        return jnp.concatenate([ref[:, c:c + PIECE] for c in starts], axis=1)
     for s in range(4):
         tot = (slot(col_send, s) + slot(col_recv.at[0], s ^ 1)) + (slot(col_recv.at[1], s ^ 2) + slot(col_recv.at[2], s ^ 3))
+        inverse = inv_count / tot
         if s < 2:
-            col_b[:, s * ROWS:(s + 1) * ROWS] = inv_count / tot
+            col_b[:, s * ROWS:(s + 1) * ROWS] = inverse
         else:
-            for k in range(STEPS):
-                start = X_BASE + (2 * k + s - 2) * CHUNK
-                col_b[:, start:start + CHUNK] = inv_count / tot[:, k * CHUNK:(k + 1) * CHUNK]
+            for p in range(ROWS // PIECE):
+                start = X_BASE + (2 * p + s - 2) * PIECE
+                col_b[:, start:start + PIECE] = inverse[:, p * PIECE:(p + 1) * PIECE]
 
     def d_img_chunk(r0):
         rows = pl.ds(r0, CHUNK)
@@ -151,17 +179,18 @@
         for j in range(TXTS // 512):
             g = [exps[rows, c:c + 128] * (row_a[rows, :] + col_b[:, c:c + 128]) for c in range(j * 512, (j + 1) * 512, 128)]
             g = jnp.concatenate([v.astype(BF16) for v in g], axis=1)
-            part = jnp.dot(g, txt[j * 512:(j + 1) * 512, :], preferred_element_type=F32)
+            texts = txt[j // 2, j % 2 * 512:(j % 2 + 1) * 512, :] if j < 4 else far[2 * j - 8:2 * j - 6].reshape(512, DIM)
+            part = jnp.dot(g, texts, preferred_element_type=F32)
             total = part if total is None else total + part
         return total
 
-    def d_txt_chunk(c0):
+    def d_txt_chunk(starts):
         total = None
         for i in range(IMGS // 512):
             rows = slice(i * 512, (i + 1) * 512)
             g = []
-            for q in range(CHUNK // 128):
-                cols = pl.ds(c0 + q * 128, 128)
+            for start in starts:
+                cols = pl.ds(start, PIECE)
                 g.append((exps[rows, cols] * (row_a[rows, :] + col_b[:, cols])).astype(BF16))
             g = jnp.concatenate(g, axis=1)
             part = lax.dot_general(g, img[rows, :], (((0,), (0,)), ((), ())), preferred_element_type=F32)
@@ -188,14 +217,15 @@
     def far_body(k, carry):
         part = chunk_of(k)
         x_cols = pl.multiple_of(X_BASE + 2 * k * CHUNK, CHUNK)
+        same, other = (x_cols, x_cols + 2 * PIECE), (x_cols + PIECE, x_cols + 3 * PIECE)
         @pl.when(k >= 2)
         def _():
             send_p(k - 2, 0, d_txt_x).wait_send()
-        ring[lax.rem(k, 2)] = d_txt_chunk(x_cols + CHUNK)
+        ring[lax.rem(k, 2)] = d_txt_chunk(other)
         send_p(k, 0, d_txt_x).start()
         d_img_send[part, :] = d_img_chunk(pl.multiple_of(ROWS + k * CHUNK, CHUNK))
         send_y(k).start()
-        mine = d_txt_chunk(x_cols)
+        mine = d_txt_chunk(same)
         send_p(k, 0, d_txt_x).wait_recv()
         d_txt_x[part, :] += mine
         send_x(k).start()
@@ -229,10 +259,11 @@
         @pl.when(k >= 2)
         def _():
             send_p(k - 2, 1, d_txt_p).wait_send()
-        ring[lax.rem(k, 2)] = d_txt_chunk(pl.multiple_of(ROWS + k * CHUNK, CHUNK))
+        first = pl.multiple_of(k * CHUNK, CHUNK)
+        ring[lax.rem(k, 2)] = d_txt_chunk((ROWS + first, ROWS + first + PIECE))
         send_p(k, 1, d_txt_p).start()
-        d_img_own[part, :] = d_img_chunk(pl.multiple_of(k * CHUNK, CHUNK))
-        mine = d_txt_chunk(pl.multiple_of(k * CHUNK, CHUNK))
+        d_img_own[part, :] = d_img_chunk(first)
+        mine = d_txt_chunk((first, first + PIECE))
         send_p(k, 1, d_txt_p).wait_recv()
         d_txt_p[part, :] += mine
         return carry
@@ -244,31 +275,25 @@
     swap_s = to_y(scal_y.at[0], scal_y.at[1], sc_ssem.at[3], sc_rsem.at[3])
     swap_s.start()
 
-    outs = []
-    for k in range(STEPS):
-        part = pl.ds(k * CHUNK, CHUNK)
-        slot_k = k % 2
-        if k >= 2:
-            outs[2 * k - 4].wait()
-            outs[2 * k - 3].wait()
+    def out_body(k, carry):
+        part = chunk_of(k)
         send_y(k).wait_recv()
-        out_stage[slot_k, 0] = (scale * (d_img_own[part, :] + d_img_recv[part, :])).astype(BF16)
-        outs.append(pltpu.make_async_copy(out_stage.at[slot_k, 0], dimg_hbm.at[part], out_sem.at[2 * k]))
-        outs[2 * k].start()
+        dimg_ref[part, :] = (scale * (d_img_own[part, :] + d_img_recv[part, :])).astype(BF16)
         send_x(k).wait_recv()
-        out_stage[slot_k, 1] = (scale * (d_txt_p[part, :] + d_txt_recv[part, :])).astype(BF16)
-        outs.append(pltpu.make_async_copy(out_stage.at[slot_k, 1], dtxt_hbm.at[part], out_sem.at[2 * k + 1]))
-        outs[2 * k + 1].start()
+        dtxt_ref[part, :] = (scale * (d_txt_p[part, :] + d_txt_recv[part, :])).astype(BF16)
+        return carry
+    lax.fori_loop(0, STEPS, out_body, 0)
 
     swap_s.wait_recv()
     total = scal_y[0] + scal_y[1]
     loss_ref[0, 0] = total[0, 0]
     dscale_ref[0, 0] = total[0, 1]
 
-    for k in range(STEPS):
+    for k in range(G_STEPS):
         gather_x[k].wait_send()
         gather_y[k].wait_send()
         relay[k].wait_send()
+    for k in range(STEPS):
         send_y(k).wait_send()
         send_x(k).wait_send()
     gather_p.wait_send()
@@ -279,8 +304,6 @@
     swap_s.wait_send()
     for k in range(STEPS - 2, STEPS):
         send_p(k, 1, d_txt_p).wait_send()
-    for k in range(2 * STEPS - 4, 2 * STEPS):
-        outs[k].wait()
 
 
 def solution(mesh):
@@ -291,20 +314,23 @@
 
     def local_tile(img_loc, txt_loc, log_scale):
         any_spec = pl.BlockSpec(memory_space=pl.ANY)
+        vmem_spec = pl.BlockSpec(memory_space=pltpu.VMEM)
         smem_spec = pl.BlockSpec(memory_space=pltpu.SMEM)
         loss, d_img, d_txt, d_scale = pl.pallas_call(
             functools.partial(kernel, inv_count),
             out_shape=(
                 jax.ShapeDtypeStruct((1, 1), F32),
-                jax.ShapeDtypeStruct((ROWS, DIM), BF16),
-                jax.ShapeDtypeStruct((ROWS, DIM), BF16),
+                pltpu.VMEM((ROWS, DIM), BF16),
+                pltpu.VMEM((ROWS, DIM), BF16),
                 jax.ShapeDtypeStruct((1, 1), F32),
             ),
             in_specs=[smem_spec, any_spec, any_spec],
-            out_specs=(smem_spec, any_spec, any_spec, smem_spec),
+            out_specs=(smem_spec, vmem_spec, vmem_spec, smem_spec),
             scratch_shapes=[
                 pltpu.VMEM((IMGS, DIM), BF16),
-                pltpu.VMEM((TXTS, DIM), BF16),
+                pltpu.VMEM((2, ROWS, DIM), BF16),
+                pltpu.VMEM((ROWS // PIECE, 2, PIECE, DIM), BF16),
+                pltpu.VMEM((DIM, TXTS), BF16),
                 pltpu.VMEM((IMGS, TXTS), F32),
                 pltpu.VMEM((IMGS, 128), F32),
                 pltpu.VMEM((IMGS, 128), F32),
@@ -322,24 +348,22 @@
                 pltpu.VMEM((ROWS, DIM), F32),
                 pltpu.VMEM((ROWS, DIM), F32),
                 pltpu.VMEM((ROWS, DIM), F32),
-                pltpu.VMEM((2, 2, CHUNK, DIM), BF16),
                 pltpu.VMEM((4, 8, 128), F32),
                 pltpu.VMEM((2, 8, 128), F32),
                 dma((2,)),
-                dma((STEPS,)), dma((STEPS,)),
-                dma((STEPS,)), dma((STEPS,)),
+                dma((G_STEPS,)), dma((G_STEPS,)),
+                dma((G_STEPS,)), dma((G_STEPS,)),
                 dma((2,)),
-                dma((STEPS,)), dma((STEPS,)),
+                dma((G_STEPS,)), dma((G_STEPS,)),
                 dma((2,)),
                 dma((3,)), dma((3,)),
                 dma((STEPS,)), dma((STEPS,)),
                 dma((2 * STEPS,)), dma((2 * STEPS,)),
                 dma((STEPS,)), dma((STEPS,)),
                 dma((4,)), dma((4,)),
-                dma((2 * STEPS,)),
             ],
             compiler_params=pltpu.CompilerParams(
-                collective_id=0, has_side_effects=True, vmem_limit_bytes=67043328,
+                collective_id=0, has_side_effects=True, vmem_limit_bytes=VMEM_LIMIT,
             ),
             name="clip_loss",
         )(log_scale.reshape(1, 1), img_loc, txt_loc)

time: 96 us -> 92.2 us (0.960)
  Pallas kernels: 87.8 us -> 85.4 us
  local copies, waits for them, and re-layouts: 3.32 us -> 1.94 us
    pallas_call x1, Pallas kernels: 87.8 us -> 85.4 us  [local_tile(): pl.pallas_call(functools.partial(kernel, inv_count), out_shape=(jax.Shape...]
    unnamed x4 -> x2, local copies, waits for them, and re-layouts: 3.32 us -> 1.94 us
where the time goes in v3:
time: 92.2 us; the launch traced here: 92 us
  Pallas kernels  85.4 us (93%)
  between operations  4.74 us (5%)
  local copies, waits for them, and re-layouts  1.94 us (2%)
    pallas_call x1, Pallas kernels, local_tile(): pl.pallas_call(functools.partial(kernel, inv_count), out_shape=(jax.Shape...  85.4 us
    unnamed x2, local copies, waits for them, and re-layouts  1.94 us

profile of v3, /device:TPU:0, one launch (start us, length us, event | category | flops | bytes accessed | tf_op | source)
XLA Modules:
  0.0 92.0 jit_solution(6217679528579906455)
XLA Ops:
  1.3 85.4 %clip_loss.1 = (f32[1,1]{1,0:T(1,128)}, bf16[1024,512]{1,0:T(8,128)(2,1)S(1)}, bf16[1024,512]{1,0:T(8,128)(2,1)S(1)}, f32[1,1]{1,0:T(1,128)}) custom-call(f32[1,1]{1,0:T(1,128)} %bitcast.3.scale_ref, bf16[1024,512]{1,0:T(8,128)(2,1)} %img_hbm.1, bf16[1024,512]{1,0:T(8,128)(2,1)} %txt_hbm.1), custom_call_target="tpu_custom_call" | custom-call | tf_op jit(solution)/shard_map/clip_loss/pallas_call | solution.py:319
  86.6 1.0 %copy.11 = bf16[1024,512]{1,0:T(8,128)(2,1)} copy(bf16[1024,512]{1,0:T(8,128)(2,1)S(1)} %get-tuple-element.13) | data formatting | bytes 2097152
  87.6 1.0 %copy.12 = bf16[1024,512]{1,0:T(8,128)(2,1)} copy(bf16[1024,512]{1,0:T(8,128)(2,1)S(1)} %get-tuple-element.14) | data formatting | bytes 2097152
